TPU v7x, 128 devices: a whole 4x4x4 slice. The times are simulated.
128 devices in a mesh: chain: 64 (over z, x_hi, y, core), aux: 2 (over x_lo).
Axes of the slice: x: 4 (x_hi: 2, x_lo: 2; x = x_hi * 2 + x_lo), y: 4, z: 4, core: 2. Of those that a mesh axis runs over, the one named last changes fastest.
Arguments:
- occupied: bfloat16 [8192, 1152], P('chain'), may hold values from -0.1875 to 0.1875
- virtual: bfloat16 [8192, 1152], P('chain'), may hold values from -0.1875 to 0.1875
- three_centre: bfloat16 [32, 8192, 1152], P('aux', 'chain'), may hold values from -6 to 6
- kernel: bfloat16 [32, 32], P('aux'), may hold values from -1 to 1
- profile: int32 [64], replicated, may hold values from 2 to 4
- atom_map: int32 [32], P('aux'), may hold values from 0 to 63
Outputs:
- band_gradient: float32 [8192, 1152], P(('chain', 'aux'))
- polarization: float32 [32, 32], P('aux')
All inputs are finite; a program needn't handle non-finite values.
Results may differ from a plain program's by a relative error of at most 0.0042.
Values may be sent and summed in bfloat16 or wider, within the bound.
A program may use at most 128 MiB of HBM per device.

v0:
```python
import math
import jax
import jax.numpy as jnp
from jax import lax
from jax.sharding import PartitionSpec as P


def passed_along(block, axis, distance):
    devices = range(lax.axis_size(axis))
    route = [(i - distance, i) for i in devices if i - distance in devices]
    return lax.ppermute(block, axis, route)


def from_everyone(shard, axis):
    size = lax.axis_size(axis)
    return lax.all_to_all(
        jnp.broadcast_to(shard[None], (size, *shard.shape)), axis, 0, 0, tiled=True
    )


def taken_together(shard, axis):
    everything = from_everyone(shard, axis)
    return jnp.sum(everything, axis=0)


def cut_along(shard, dim, size):
    before, after = (shard.shape[:dim], shard.shape[dim + 1 :])
    return jnp.moveaxis(shard.reshape(*before, size, -1, *after), dim, 0)


def sent_and_summed(shard, axis, dim):
    parts = cut_along(shard, dim, lax.axis_size(axis))
    arrived = lax.all_to_all(parts, axis, split_axis=0, concat_axis=0, tiled=True)
    return arrived.sum(axis=0)


def shift_blocks(matrix, offset, block_size):
    if offset == 0:
        return matrix
    padding = jnp.zeros(matrix.shape[:-1] + (abs(offset) * block_size,), matrix.dtype)
    if offset > 0:
        return jnp.concatenate([padding, matrix[..., : -offset * block_size]], -1)
    return jnp.concatenate([matrix[..., -offset * block_size :], padding], -1)


def body(occupied, virtual, three_centre, kernel, profile, atom_map):
    block_size = occupied.shape[0]
    band_cols = occupied.shape[1]
    slots_total = band_cols // block_size
    spread = (slots_total - 1) // 2
    nblocks = lax.axis_size("chain")
    position = lax.axis_index("chain")
    slot_ids = jnp.arange(slots_total, dtype=jnp.int32)
    block_ids = jnp.arange(nblocks, dtype=jnp.int32)
    others = position + slot_ids - spread
    neighbours = jnp.sum(jnp.where(block_ids[None, :] == others[:, None], profile[None, :], 0), 1)
    own_width = jnp.sum(jnp.where(block_ids == position, profile, 0))
    allowed = jnp.abs(slot_ids - spread) <= jnp.minimum(own_width, neighbours)
    column_keep = jnp.repeat(allowed, block_size)
    zero_half = jnp.zeros((), jnp.bfloat16)
    occ_masked = jnp.where(column_keep[None, :], occupied, zero_half)
    vir_masked = jnp.where(column_keep[None, :], virtual, zero_half)
    both_bands = jnp.stack([occ_masked, vir_masked])
    fetched = []
    for slot_index in range(slots_total):
        if slot_index == spread:
            fetched.append(both_bands)
        else:
            fetched.append(passed_along(both_bands, "chain", spread - slot_index))
    stack_occ = jnp.concatenate(
        [shift_blocks(fetched[k][0], k - spread, block_size) for k in range(slots_total)], 0
    )
    stack_vir = jnp.concatenate(
        [shift_blocks(fetched[k][1], k - spread, block_size) for k in range(slots_total)], 0
    )
    aux_here = three_centre.shape[0]
    aux_total = kernel.shape[1]
    screen = jnp.abs(atom_map - position) <= nblocks // 4
    local = jnp.where(column_keep[None, None, :] & screen[:, None, None], three_centre, zero_half)
    screened = local.reshape(aux_here * block_size, band_cols)
    coupled = jnp.dot(screened, stack_occ, preferred_element_type=jnp.float32).astype(jnp.bfloat16)
    coupled = coupled.reshape(aux_here, block_size * band_cols)
    partner = jnp.dot(screened, stack_vir, preferred_element_type=jnp.float32).astype(jnp.bfloat16)
    partner = partner.reshape(aux_here, block_size, band_cols)
    piece = lax.all_gather(partner, "aux", axis=0, tiled=True)
    piece_rows = piece.shape[0]
    columns = piece.reshape(piece_rows, block_size * band_cols)
    products = lax.dot_general(
        coupled, columns, (((1,), (1,)), ((), ())), preferred_element_type=jnp.float32
    )
    polar_part = products
    response_sum = jnp.dot(kernel, columns, preferred_element_type=jnp.float32)
    polar_part, response_sum = (polar_part, response_sum)
    polarization = taken_together(polar_part, "chain") * (
        1.0 / math.sqrt(block_size * nblocks * band_cols)
    )
    response = response_sum.astype(jnp.bfloat16).reshape(aux_here * block_size, band_cols)
    partials = lax.dot_general(
        screened, response, (((0,), (0,)), ((), ())), preferred_element_type=jnp.float32
    )
    partials = partials.reshape(slots_total, block_size, band_cols)
    gathered_sum = partials[spread]
    for slot_index in range(slots_total):
        if slot_index != spread:
            moved = shift_blocks(partials[slot_index], spread - slot_index, block_size)
            gathered_sum = gathered_sum + passed_along(
                moved.astype(jnp.bfloat16), "chain", slot_index - spread
            ).astype(moved.dtype)
    gathered_sum = sent_and_summed(gathered_sum, "aux", 0)
    scale_grad = 1.0 / math.sqrt(block_size * aux_total)
    band_gradient = (
        jnp.where(column_keep[None, :], gathered_sum, jnp.zeros((), jnp.float32)) * scale_grad
    )
    return (band_gradient, polarization)


def solution(mesh):
    placed = (
        P("chain", None),
        P("chain", None),
        P("aux", "chain", None),
        P("aux", None),
        P(),
        P("aux"),
    )
    return jax.shard_map(
        body,
        mesh=mesh,
        in_specs=placed,
        out_specs=(P(("chain", "aux"), None), P("aux", None)),
        check_vma=False,
    )
```

profile of v0, /device:TPU:1, one launch (start us, length us, event | category | flops | bytes accessed | tf_op | source)
XLA Modules:
  0.0 339.7 jit_solution(14269273563489841605)
XLA Ops:
  7.2 0.0 all-gather.2.cloned.1.call-start
  7.2 1.3 fusion.12
  8.5 0.8 select_reduce_fusion
  9.4 0.7 minimum_compare_fusion
  10.0 0.1 broadcast_bitcast_fusion
  10.1 1.1 fusion.9
  11.2 0.1 pad_maximum_fusion
  11.3 5.7 %collective-permute-start = (bf16[2,128,1152]{2,1,0:T(8,128)(2,1)S(1)}, bf16[2,128,1152]{2,1,0:T(8,128)(2,1)S(1)}, u32[]{:S(2)}, u32[]{:S(2)}) collective-permute-start(bf16[2,128,1152]{2,1,0:T(8,128)(2,1)S(1)} %pad_maximum_fusion), channel_id=1, source_target_pairs={{0,8},{2,10},{4,12},{6,14},{8,16},{10,18},{12,20},{14,22},{16,24},... | collective-permute-start | bytes 1769480 | tf_op jit(solution)/shard_map/ppermute | solution.py:11
  17.0 5.3 %collective-permute-start.1 = (bf16[2,128,1152]{2,1,0:T(8,128)(2,1)S(1)}, bf16[2,128,1152]{2,1,0:T(8,128)(2,1)S(1)}, u32[]{:S(2)}, u32[]{:S(2)}) collective-permute-start(bf16[2,128,1152]{2,1,0:T(8,128)(2,1)S(1)} %pad_maximum_fusion), channel_id=1, source_target_pairs={{0,6},{2,8},{4,10},{6,12},{8,14},{10,16},{12,18},{14,20},{16,22},{... | collective-permute-start | bytes 1769480 | tf_op jit(solution)/shard_map/ppermute | solution.py:11
  22.2 3.2 collective-permute-start.2
  25.5 1.9 collective-permute-start.3
  27.4 2.4 collective-permute-start.4
  29.8 0.7 abs_compare_fusion
  30.5 0.1 broadcast_and_fusion
  30.6 2.8 broadcast_select_fusion
  33.4 1.3 collective-permute-start.5
  34.8 6.8 %collective-permute-done.1 = bf16[2,128,1152]{2,1,0:T(8,128)(2,1)S(1)} collective-permute-done((bf16[2,128,1152]{2,1,0:T(8,128)(2,1)S(1)}, bf16[2,128,1152]{2,1,0:T(8,128)(2,1)S(1)}, u32[]{:S(2)}, u32[]{:S(2)}) %collective-permute-start.1) | collective-permute-done | bytes 589856 | tf_op jit(solution)/shard_map/ppermute | solution.py:11
  41.6 1.3 collective-permute-start.6
  43.0 11.3 %collective-permute-done.2 = bf16[2,128,1152]{2,1,0:T(8,128)(2,1)S(1)} collective-permute-done((bf16[2,128,1152]{2,1,0:T(8,128)(2,1)S(1)}, bf16[2,128,1152]{2,1,0:T(8,128)(2,1)S(1)}, u32[]{:S(2)}, u32[]{:S(2)}) %collective-permute-start.2) | collective-permute-done | bytes 589856 | tf_op jit(solution)/shard_map/ppermute | solution.py:11
  54.3 1.3 collective-permute-start.7
  55.6 8.8 %collective-permute-done.3 = bf16[2,128,1152]{2,1,0:T(8,128)(2,1)S(1)} collective-permute-done((bf16[2,128,1152]{2,1,0:T(8,128)(2,1)S(1)}, bf16[2,128,1152]{2,1,0:T(8,128)(2,1)S(1)}, u32[]{:S(2)}, u32[]{:S(2)}) %collective-permute-start.3) | collective-permute-done | bytes 589856 | tf_op jit(solution)/shard_map/ppermute | solution.py:11
  64.5 14.6 %collective-permute-done.6 = bf16[2,128,1152]{2,1,0:T(8,128)(2,1)S(1)} collective-permute-done((bf16[2,128,1152]{2,1,0:T(8,128)(2,1)S(1)}, bf16[2,128,1152]{2,1,0:T(8,128)(2,1)S(1)}, u32[]{:S(2)}, u32[]{:S(2)}) %collective-permute-start.6) | collective-permute-done | bytes 589856 | tf_op jit(solution)/shard_map/ppermute | solution.py:11
  79.9 0.6 copy-done.2
  80.5 0.1 copy-done.3
  80.6 0.1 fusion.8
  80.8 0.1 pad_dynamic-update-slice_fusion.3
  81.0 8.5 %convolution_convert_fusion.2 = bf16[2048,1152]{1,0:T(8,128)(2,1)} fusion(bf16[2048,1152]{1,0:T(8,128)(2,1)S(1)} %bitcast.61, bf16[1152,1152]{1,0:T(8,128)(2,1)S(1)} %pad_dynamic-update-slice_fusion.8), kind=kOutput, calls=%fused_computation.3 | convolution fusion | flops 5438177280 | bytes 12091392 | tf_op jit(solution)/shard_map/dot_general | solution.py:83
  89.6 0.7 pad_dynamic-update-slice_fusion.2
  90.4 0.7 pad_dynamic-update-slice_fusion.1
  91.1 0.7 pad_dynamic-update-slice_fusion
  91.8 10.9 %convolution_convert_fusion.1 = bf16[2048,1152]{1,0:T(8,128)(2,1)} fusion(bf16[2048,1152]{1,0:T(8,128)(2,1)} %bitcast.62, bf16[1152,1152]{1,0:T(8,128)(2,1)} %pad_dynamic-update-slice_fusion), kind=kOutput, calls=%fused_computation.2 | convolution fusion | flops 5438177280 | bytes 12091392 | tf_op jit(solution)/shard_map/dot_general | solution.py:81
  102.7 5.2 %reshape.85 = bf16[16,147456]{1,0:T(8,128)(2,1)} reshape(bf16[2048,1152]{1,0:T(8,128)(2,1)} %convolution_convert_fusion.1) | data formatting | bytes 9437184 | tf_op jit(solution)/shard_map/reshape | solution.py:82
  107.9 110.5 %all-gather.2.cloned.1.call-done = bf16[32,128,1152]{2,1,0:T(8,128)(2,1)} async-done(((bf16[16,128,1152]{2,1,0:T(8,128)(2,1)}), bf16[32,128,1152]{2,1,0:T(8,128)(2,1)}) %all-gather.2.cloned.1.call-update) | async-done | bytes 9437200 | tf_op jit(solution)/shard_map/all_gather | solution.py:85
  218.4 12.7 %copy.10 = bf16[4,8,128,1152]{3,1,2,0:T(8,128)(2,1)} copy(bf16[4,8,128,1152]{3,2,1,0:T(8,128)(2,1)} %bitcast.59) | data formatting | bytes 18874368
  231.2 7.2 %fusion = bf16[16,147456]{1,0:T(8,128)(2,1)} fusion(bf16[16,32]{1,0:T(8,128)(2,1)S(1)} %copy-done, bf16[32,147456]{1,0:T(8,128)(2,1)} %bitcast.55), kind=kOutput, calls=%fused_computation.1 | convolution fusion | flops 153354240 | bytes 14156800 | tf_op jit(solution)/shard_map/dot_general | solution.py:92
  238.4 5.3 %reshape.83 = bf16[2048,1152]{1,0:T(8,128)(2,1)} reshape(bf16[16,147456]{1,0:T(8,128)(2,1)} %fusion) | data formatting | bytes 9437184 | tf_op jit(solution)/shard_map/reshape | solution.py:97
  243.7 12.6 %fusion.17 = (bf16[1152,1152]{1,0:T(8,128)(2,1)S(1)}, f32[1152,1152]{1,0:T(8,128)}) fusion(bf16[2048,1152]{1,0:T(8,128)(2,1)} %bitcast.63, bf16[2048,1152]{1,0:T(8,128)(2,1)} %reshape.83), kind=kOutput, calls=%fused_computation.67 | convolution fusion | flops 5437145088 | bytes 17399808 | tf_op jit(solution)/shard_map/dot_general | solution.py:98
  256.3 0.1 fusion.16
  256.4 2.7 collective-permute-start.11
  259.2 3.0 collective-permute-start.12
  262.3 1.3 collective-permute-start.10
  263.6 0.7 concatenate.92
  264.3 4.0 %collective-permute-start.13 = (bf16[128,1152]{1,0:T(8,128)(2,1)}, bf16[128,1152]{1,0:T(8,128)(2,1)S(1)}, u32[]{:S(2)}, u32[]{:S(2)}) collective-permute-start(bf16[128,1152]{1,0:T(8,128)(2,1)} %concatenate.92), channel_id=1, source_target_pairs={{0,4},{2,6},{4,8},{6,10},{8,12},{10,14},{12,16},{14,18},{16,20},{1... | collective-permute-start | bytes 884744 | tf_op jit(solution)/shard_map/ppermute | solution.py:11
  268.3 0.7 concatenate.93
  269.1 4.5 %collective-permute-start.14 = (bf16[128,1152]{1,0:T(8,128)(2,1)}, bf16[128,1152]{1,0:T(8,128)(2,1)S(1)}, u32[]{:S(2)}, u32[]{:S(2)}) collective-permute-start(bf16[128,1152]{1,0:T(8,128)(2,1)} %concatenate.93), channel_id=1, source_target_pairs={{0,6},{2,8},{4,10},{6,12},{8,14},{10,16},{12,18},{14,20},{16,22},{... | collective-permute-start | bytes 884744 | tf_op jit(solution)/shard_map/ppermute | solution.py:11
  273.5 0.7 concatenate.88
  274.3 0.7 concatenate.94
  275.0 0.7 concatenate.87
  275.8 1.3 collective-permute-start.9
  277.1 7.3 %collective-permute-start.15 = (bf16[128,1152]{1,0:T(8,128)(2,1)}, bf16[128,1152]{1,0:T(8,128)(2,1)S(1)}, u32[]{:S(2)}, u32[]{:S(2)}) collective-permute-start(bf16[128,1152]{1,0:T(8,128)(2,1)} %concatenate.94), channel_id=1, source_target_pairs={{0,8},{2,10},{4,12},{6,14},{8,16},{10,18},{12,20},{14,22},{16,24},... | collective-permute-start | bytes 884744 | tf_op jit(solution)/shard_map/ppermute | solution.py:11
  284.4 1.3 collective-permute-start.8
  285.8 4.3 %fusion.18 = f32[16,32]{1,0:T(8,128)S(1)} fusion(bf16[16,147456]{1,0:T(8,128)(2,1)} %reshape.85, bf16[32,147456]{1,0:T(8,128)(2,1)S(1)} %bitcast.58), kind=kOutput, calls=%fused_computation.68 | convolution fusion | flops 150994944 | bytes 14157824 | tf_op jit(solution)/shard_map/dot_general | solution.py:88
  290.2 0.9 reshape.86
  291.1 19.2 %all-to-all-start.1 = ((f32[64,1,512]{2,1,0:T(1,128)}), f32[64,1,512]{2,1,0:T(1,128)S(1)}, u32[]{:S(2)}, u32[]{:S(2)}) async-start(f32[64,1,512]{2,1,0:T(1,128)} %reshape.86), calls=%async_computation.1 | async-start | bytes 262144 | tf_op jit(solution)/shard_map/all_to_all | solution.py:16
  310.3 2.2 fusion.7
  312.5 7.8 %all-to-all-done.1 = f32[64,1,512]{2,1,0:T(1,128)S(1)} async-done(((f32[64,1,512]{2,1,0:T(1,128)}), f32[64,1,512]{2,1,0:T(1,128)S(1)}, u32[]{:S(2)}, u32[]{:S(2)}) %all-to-all-start.1) | async-done | bytes 131104 | tf_op jit(solution)/shard_map/all_to_all | solution.py:16
  320.2 3.5 %all-to-all-start = ((f32[2,64,1152]{2,1,0:T(8,128)}), f32[2,64,1152]{2,1,0:T(8,128)S(1)}, u32[]{:S(2)}, u32[]{:S(2)}) async-start(f32[2,64,1152]{2,1,0:T(8,128)} %bitcast.14), calls=%async_computation | async-start | bytes 1179648 | tf_op jit(solution)/shard_map/all_to_all | solution.py:33
  323.7 0.5 broadcast.96
  324.3 1.0 reduce
  325.2 0.2 reshape.87
  325.4 0.1 reduce_sum.39
  325.5 0.6 broadcast_multiply_fusion
  326.1 6.0 %all-to-all-done = f32[2,64,1152]{2,1,0:T(8,128)S(1)} async-done(((f32[2,64,1152]{2,1,0:T(8,128)}), f32[2,64,1152]{2,1,0:T(8,128)S(1)}, u32[]{:S(2)}, u32[]{:S(2)}) %all-to-all-start) | async-done | bytes 589856 | tf_op jit(solution)/shard_map/all_to_all | solution.py:33
  332.1 0.7 select_multiply_fusion
  (72 shorter events, 1.3 us)
Async XLA Ops:
  7.2 224.0 %copy-start = (bf16[16,32]{1,0:T(8,128)(2,1)S(1)}, bf16[16,32]{1,0:T(8,128)(2,1)}, u32[]{:S(2)}) copy-start(bf16[16,32]{1,0:T(8,128)(2,1)} %param.9) | copy-start | bytes 3076
  7.2 211.3 %all-gather.2.cloned.1.call-start = ((), (), s32[]{:S(2)}) async-start(), calls=%async_computation.2 | async-start | bytes 14155776 | tf_op jit(solution)/shard_map/all_gather | solution.py:85
  11.3 22.1 %collective-permute-start = (bf16[2,128,1152]{2,1,0:T(8,128)(2,1)S(1)}, bf16[2,128,1152]{2,1,0:T(8,128)(2,1)S(1)}, u32[]{:S(2)}, u32[]{:S(2)}) collective-permute-start(bf16[2,128,1152]{2,1,0:T(8,128)(2,1)S(1)} %pad_maximum_fusion), channel_id=1, source_target_pairs={{0,8},{2,10},{4,12},{6,14},{8,16},{10,18},{12,20},{14,22},{16,24},... | collective-permute-start | bytes 1769480 | tf_op jit(solution)/shard_map/ppermute | solution.py:11
  17.0 24.6 %collective-permute-start.1 = (bf16[2,128,1152]{2,1,0:T(8,128)(2,1)S(1)}, bf16[2,128,1152]{2,1,0:T(8,128)(2,1)S(1)}, u32[]{:S(2)}, u32[]{:S(2)}) collective-permute-start(bf16[2,128,1152]{2,1,0:T(8,128)(2,1)S(1)} %pad_maximum_fusion), channel_id=1, source_target_pairs={{0,6},{2,8},{4,10},{6,12},{8,14},{10,16},{12,18},{14,20},{16,22},{... | collective-permute-start | bytes 1769480 | tf_op jit(solution)/shard_map/ppermute | solution.py:11
  22.2 32.0 %collective-permute-start.2 = (bf16[2,128,1152]{2,1,0:T(8,128)(2,1)S(1)}, bf16[2,128,1152]{2,1,0:T(8,128)(2,1)S(1)}, u32[]{:S(2)}, u32[]{:S(2)}) collective-permute-start(bf16[2,128,1152]{2,1,0:T(8,128)(2,1)S(1)} %pad_maximum_fusion), channel_id=1, source_target_pairs={{0,4},{2,6},{4,8},{6,10},{8,12},{10,14},{12,16},{14,18},{16,20},{1... | collective-permute-start | bytes 1769480 | tf_op jit(solution)/shard_map/ppermute | solution.py:11
  25.5 38.9 %collective-permute-start.3 = (bf16[2,128,1152]{2,1,0:T(8,128)(2,1)S(1)}, bf16[2,128,1152]{2,1,0:T(8,128)(2,1)S(1)}, u32[]{:S(2)}, u32[]{:S(2)}) collective-permute-start(bf16[2,128,1152]{2,1,0:T(8,128)(2,1)S(1)} %pad_maximum_fusion), channel_id=1, source_target_pairs={{0,2},{2,4},{4,6},{6,8},{8,10},{10,12},{12,14},{14,16},{16,18},{18... | collective-permute-start | bytes 1769480 | tf_op jit(solution)/shard_map/ppermute | solution.py:11
  27.4 37.0 %collective-permute-start.4 = (bf16[2,128,1152]{2,1,0:T(8,128)(2,1)S(1)}, bf16[2,128,1152]{2,1,0:T(8,128)(2,1)S(1)}, u32[]{:S(2)}, u32[]{:S(2)}) collective-permute-start(bf16[2,128,1152]{2,1,0:T(8,128)(2,1)S(1)} %pad_maximum_fusion), channel_id=1, source_target_pairs={{2,0},{4,2},{6,4},{8,6},{10,8},{12,10},{14,12},{16,14},{18,16},{20... | collective-permute-start | bytes 1769480 | tf_op jit(solution)/shard_map/ppermute | solution.py:11
  33.4 47.6 %copy-start.1 = (bf16[16,128,1152]{2,1,0:T(8,128)(2,1)}, bf16[16,128,1152]{2,1,0:T(8,128)(2,1)S(1)}, u32[]{:S(2)}) copy-start(bf16[16,128,1152]{2,1,0:T(8,128)(2,1)S(1)} %broadcast_select_fusion) | copy-start | bytes 14155780
  33.4 31.0 %collective-permute-start.5 = (bf16[2,128,1152]{2,1,0:T(8,128)(2,1)S(1)}, bf16[2,128,1152]{2,1,0:T(8,128)(2,1)S(1)}, u32[]{:S(2)}, u32[]{:S(2)}) collective-permute-start(bf16[2,128,1152]{2,1,0:T(8,128)(2,1)S(1)} %pad_maximum_fusion), channel_id=1, source_target_pairs={{4,0},{6,2},{8,4},{10,6},{12,8},{14,10},{16,12},{18,14},{20,16},{2... | collective-permute-start | bytes 1769480 | tf_op jit(solution)/shard_map/ppermute | solution.py:11
  41.6 37.6 %collective-permute-start.6 = (bf16[2,128,1152]{2,1,0:T(8,128)(2,1)S(1)}, bf16[2,128,1152]{2,1,0:T(8,128)(2,1)S(1)}, u32[]{:S(2)}, u32[]{:S(2)}) collective-permute-start(bf16[2,128,1152]{2,1,0:T(8,128)(2,1)S(1)} %pad_maximum_fusion), channel_id=1, source_target_pairs={{6,0},{8,2},{10,4},{12,6},{14,8},{16,10},{18,12},{20,14},{22,16},{... | collective-permute-start | bytes 1769480 | tf_op jit(solution)/shard_map/ppermute | solution.py:11
  54.3 25.4 %collective-permute-start.7 = (bf16[2,128,1152]{2,1,0:T(8,128)(2,1)S(1)}, bf16[2,128,1152]{2,1,0:T(8,128)(2,1)S(1)}, u32[]{:S(2)}, u32[]{:S(2)}) collective-permute-start(bf16[2,128,1152]{2,1,0:T(8,128)(2,1)S(1)} %pad_maximum_fusion), channel_id=1, source_target_pairs={{8,0},{10,2},{12,4},{14,6},{16,8},{18,10},{20,12},{22,14},{24,16},... | collective-permute-start | bytes 1769480 | tf_op jit(solution)/shard_map/ppermute | solution.py:11
  79.6 1.0 copy-start.2
  79.6 1.0 copy-start.3
  80.9 8.7 %copy-start.4 = (bf16[1152,1152]{1,0:T(8,128)(2,1)}, bf16[1152,1152]{1,0:T(8,128)(2,1)S(1)}, u32[]{:S(2)}) copy-start(bf16[1152,1152]{1,0:T(8,128)(2,1)S(1)} %get-tuple-element.32) | copy-start | bytes 7962628
  238.4 47.3 %slice-start = ((s8[9437184]{0:T(1024)(128)(4,1)}), s8[1048576]{0:T(1024)(128)(4,1)S(1)}, s32[]{:S(2)}) async-start(s8[9437184]{0:T(1024)(128)(4,1)} %bitcast.56), calls=%async_computation.3 | async-start | bytes 2097152
  243.7 42.1 %slice-start.1 = ((s8[9437184]{0:T(1024)(128)(4,1)}), s8[4194304]{0:T(1024)(128)(4,1)S(1)}, s32[]{:S(2)}) async-start(s8[9437184]{0:T(1024)(128)(4,1)} %bitcast.56), calls=%async_computation.4 | async-start | bytes 8388608
  243.7 42.1 %slice-start.2 = ((s8[9437184]{0:T(1024)(128)(4,1)}), s8[4194304]{0:T(1024)(128)(4,1)S(1)}, s32[]{:S(2)}) async-start(s8[9437184]{0:T(1024)(128)(4,1)} %bitcast.56), calls=%async_computation.5 | async-start | bytes 8388608
  256.4 19.4 %collective-permute-start.11 = (bf16[128,1152]{1,0:T(8,128)(2,1)S(1)}, bf16[128,1152]{1,0:T(8,128)(2,1)S(1)}, u32[]{:S(2)}, u32[]{:S(2)}) collective-permute-start(bf16[128,1152]{1,0:T(8,128)(2,1)S(1)} %concatenate.90), channel_id=1, source_target_pairs={{2,0},{4,2},{6,4},{8,6},{10,8},{12,10},{14,12},{16,14},{18,16},{20... | collective-permute-start | bytes 884744 | tf_op jit(solution)/shard_map/ppermute | solution.py:11
  259.2 17.9 %collective-permute-start.12 = (bf16[128,1152]{1,0:T(8,128)(2,1)S(1)}, bf16[128,1152]{1,0:T(8,128)(2,1)S(1)}, u32[]{:S(2)}, u32[]{:S(2)}) collective-permute-start(bf16[128,1152]{1,0:T(8,128)(2,1)S(1)} %concatenate.91), channel_id=1, source_target_pairs={{0,2},{2,4},{4,6},{6,8},{8,10},{10,12},{12,14},{14,16},{16,18},{18... | collective-permute-start | bytes 884744 | tf_op jit(solution)/shard_map/ppermute | solution.py:11
  262.3 22.2 %collective-permute-start.10 = (bf16[128,1152]{1,0:T(8,128)(2,1)S(1)}, bf16[128,1152]{1,0:T(8,128)(2,1)S(1)}, u32[]{:S(2)}, u32[]{:S(2)}) collective-permute-start(bf16[128,1152]{1,0:T(8,128)(2,1)S(1)} %concatenate.89), channel_id=1, source_target_pairs={{4,0},{6,2},{8,4},{10,6},{12,8},{14,10},{16,12},{18,14},{20,16},{2... | collective-permute-start | bytes 884744 | tf_op jit(solution)/shard_map/ppermute | solution.py:11
  264.3 45.9 %collective-permute-start.13 = (bf16[128,1152]{1,0:T(8,128)(2,1)}, bf16[128,1152]{1,0:T(8,128)(2,1)S(1)}, u32[]{:S(2)}, u32[]{:S(2)}) collective-permute-start(bf16[128,1152]{1,0:T(8,128)(2,1)} %concatenate.92), channel_id=1, source_target_pairs={{0,4},{2,6},{4,8},{6,10},{8,12},{10,14},{12,16},{14,18},{16,20},{1... | collective-permute-start | bytes 884744 | tf_op jit(solution)/shard_map/ppermute | solution.py:11
  269.1 41.2 %collective-permute-start.14 = (bf16[128,1152]{1,0:T(8,128)(2,1)}, bf16[128,1152]{1,0:T(8,128)(2,1)S(1)}, u32[]{:S(2)}, u32[]{:S(2)}) collective-permute-start(bf16[128,1152]{1,0:T(8,128)(2,1)} %concatenate.93), channel_id=1, source_target_pairs={{0,6},{2,8},{4,10},{6,12},{8,14},{10,16},{12,18},{14,20},{16,22},{... | collective-permute-start | bytes 884744 | tf_op jit(solution)/shard_map/ppermute | solution.py:11
  275.8 34.5 %collective-permute-start.9 = (bf16[128,1152]{1,0:T(8,128)(2,1)}, bf16[128,1152]{1,0:T(8,128)(2,1)S(1)}, u32[]{:S(2)}, u32[]{:S(2)}) collective-permute-start(bf16[128,1152]{1,0:T(8,128)(2,1)} %concatenate.88), channel_id=1, source_target_pairs={{6,0},{8,2},{10,4},{12,6},{14,8},{16,10},{18,12},{20,14},{22,16},{... | collective-permute-start | bytes 884744 | tf_op jit(solution)/shard_map/ppermute | solution.py:11
  277.1 33.2 %collective-permute-start.15 = (bf16[128,1152]{1,0:T(8,128)(2,1)}, bf16[128,1152]{1,0:T(8,128)(2,1)S(1)}, u32[]{:S(2)}, u32[]{:S(2)}) collective-permute-start(bf16[128,1152]{1,0:T(8,128)(2,1)} %concatenate.94), channel_id=1, source_target_pairs={{0,8},{2,10},{4,12},{6,14},{8,16},{10,18},{12,20},{14,22},{16,24},... | collective-permute-start | bytes 884744 | tf_op jit(solution)/shard_map/ppermute | solution.py:11
  284.4 25.9 %collective-permute-start.8 = (bf16[128,1152]{1,0:T(8,128)(2,1)}, bf16[128,1152]{1,0:T(8,128)(2,1)S(1)}, u32[]{:S(2)}, u32[]{:S(2)}) collective-permute-start(bf16[128,1152]{1,0:T(8,128)(2,1)} %concatenate.87), channel_id=1, source_target_pairs={{8,0},{10,2},{12,4},{14,6},{16,8},{18,10},{20,12},{22,14},{24,16},... | collective-permute-start | bytes 884744 | tf_op jit(solution)/shard_map/ppermute | solution.py:11
  291.1 29.2 %all-to-all-start.1 = ((f32[64,1,512]{2,1,0:T(1,128)}), f32[64,1,512]{2,1,0:T(1,128)S(1)}, u32[]{:S(2)}, u32[]{:S(2)}) async-start(f32[64,1,512]{2,1,0:T(1,128)} %reshape.86), calls=%async_computation.1 | async-start | bytes 262144 | tf_op jit(solution)/shard_map/all_to_all | solution.py:16
  320.2 11.9 %all-to-all-start = ((f32[2,64,1152]{2,1,0:T(8,128)}), f32[2,64,1152]{2,1,0:T(8,128)S(1)}, u32[]{:S(2)}, u32[]{:S(2)}) async-start(f32[2,64,1152]{2,1,0:T(8,128)} %bitcast.14), calls=%async_computation | async-start | bytes 1179648 | tf_op jit(solution)/shard_map/all_to_all | solution.py:33
Sparse Core Ops, SparseCore 0:
  89.7 128.7 all-gather.1
where the time goes:
time: 341 us; the launch traced here: 340 us
  waiting for transfers between devices  166 us (49%)
  starting transfers between devices  70.5 us (21%)
  matrix products  43.6 us (13%)
  local copies, waits for them, and re-layouts  32.8 us (10%)
  between operations  14.7 us (4%)
  other arithmetic  12.3 us (4%)
    all_gather x1, waiting for transfers between devices, body(): piece = lax.all_gather(partner, 'aux', axis=0, tiled=True)  111 us
    ppermute x16, starting transfers between devices, passed_along(): return lax.ppermute(block, axis, route)  47.8 us
    ppermute x16, waiting for transfers between devices, passed_along(): return lax.ppermute(block, axis, route)  41.6 us
    all_to_all x1, starting transfers between devices, from_everyone(): lax.all_to_all(jnp.broadcast_to(shard[None], (size, *shard.shape)), axis,...  19.2 us
    unnamed x32, local copies, waits for them, and re-layouts  16.4 us
    dot_general x1, matrix products, body(): lax.dot_general(screened, response, (((0,), (0,)), ((), ())), preferred_e...  12.6 us
    dot_general x1, matrix products, body(): jnp.dot(screened, stack_occ, preferred_element_type=jnp.float32)  10.9 us
    dot_general x1, matrix products, body(): jnp.dot(screened, stack_vir, preferred_element_type=jnp.float32)  8.54 us
  transfers between devices with their start and end apart: 19, of which 7 were waited for; matrix products, arithmetic and copies ran while one was open for 11% of the time, Pallas kernels for 0%

commit v1 on v0

--- a/solution.py
+++ b/solution.py
@@ -3,6 +3,7 @@
 import jax.numpy as jnp
 from jax import lax
 from jax.sharding import PartitionSpec as P
+from jax.lax import all_to_all, axis_size
 
 
 def passed_along(block, axis, distance):
@@ -82,7 +83,15 @@
     coupled = coupled.reshape(aux_here, block_size * band_cols)
     partner = jnp.dot(screened, stack_vir, preferred_element_type=jnp.float32).astype(jnp.bfloat16)
     partner = partner.reshape(aux_here, block_size, band_cols)
-    piece = lax.all_gather(partner, "aux", axis=0, tiled=True)
+    piece = jnp.concatenate(
+        all_to_all(
+            jnp.stack([partner for _ in range(axis_size("aux"))]),
+            "aux",
+            split_axis=0,
+            concat_axis=0,
+        ),
+        axis=0,
+    )
     piece_rows = piece.shape[0]
     columns = piece.reshape(piece_rows, block_size * band_cols)
     products = lax.dot_general(

time: 341 us -> 317 us (0.930)
  waiting for transfers between devices: 166 us -> 135 us
  between operations: 14.7 us -> 1.35 us
  starting transfers between devices: 70.5 us -> 82 us
  other arithmetic: 12.3 us -> 20.6 us
    all_gather x1 -> x0, waiting for transfers between devices: 111 us -> none  [body(): piece = lax.all_gather(partner, 'aux', axis=0, tiled=True)]
    all_to_all x0 -> x1, waiting for transfers between devices: none -> 80.1 us  [body(): all_to_all(jnp.stack([partner for _ in range(axis_size('aux'))]), 'aux',...]
    another operation x0 -> x1, other arithmetic: none -> 8.33 us  [body(): jnp.stack([partner for _ in range(axis_size('aux'))])]
    all_to_all x0 -> x1, starting transfers between devices: none -> 7.32 us  [body(): all_to_all(jnp.stack([partner for _ in range(axis_size('aux'))]), 'aux',...]
    ppermute x16, starting transfers between devices: 47.8 us -> 51.8 us  [passed_along(): return lax.ppermute(block, axis, route)]
where the time goes in v1:
time: 317 us; the launch traced here: 316 us
  waiting for transfers between devices  135 us (43%)
  starting transfers between devices  82 us (26%)
  matrix products  43.6 us (14%)
  local copies, waits for them, and re-layouts  32.8 us (10%)
  other arithmetic  20.6 us (6%)
    all_to_all x1, waiting for transfers between devices, body(): all_to_all(jnp.stack([partner for _ in range(axis_size('aux'))]), 'aux',...  80.1 us
    ppermute x16, starting transfers between devices, passed_along(): return lax.ppermute(block, axis, route)  51.8 us
    ppermute x16, waiting for transfers between devices, passed_along(): return lax.ppermute(block, axis, route)  41.6 us
    all_to_all x1, starting transfers between devices, from_everyone(): lax.all_to_all(jnp.broadcast_to(shard[None], (size, *shard.shape)), axis,...  19.4 us
    unnamed x32, local copies, waits for them, and re-layouts  16.4 us
    dot_general x1, matrix products, body(): lax.dot_general(screened, response, (((0,), (0,)), ((), ())), preferred_e...  12.6 us
    dot_general x1, matrix products, body(): jnp.dot(screened, stack_occ, preferred_element_type=jnp.float32)  10.9 us
    dot_general x1, matrix products, body(): jnp.dot(screened, stack_vir, preferred_element_type=jnp.float32)  8.55 us
  transfers between devices with their start and end apart: 19, of which 7 were waited for; matrix products, arithmetic and copies ran while one was open for 11% of the time, Pallas kernels for 0%

profile of v1, /device:TPU:1, one launch (start us, length us, event | category | flops | bytes accessed | tf_op | source)
XLA Modules:
  0.0 315.8 jit_solution(3701856207009872673)
XLA Ops:
  0.7 1.3 fusion.12
  2.0 0.8 select_reduce_fusion
  2.8 0.7 minimum_compare_fusion
  3.5 0.1 broadcast_bitcast_fusion
  3.5 1.1 fusion.9
  4.6 0.1 pad_maximum_fusion.1
  4.7 5.7 %collective-permute-start = (bf16[2,128,1152]{2,1,0:T(8,128)(2,1)S(1)}, bf16[2,128,1152]{2,1,0:T(8,128)(2,1)S(1)}, u32[]{:S(2)}, u32[]{:S(2)}) collective-permute-start(bf16[2,128,1152]{2,1,0:T(8,128)(2,1)S(1)} %pad_maximum_fusion.1), channel_id=1, source_target_pairs={{0,8},{2,10},{4,12},{6,14},{8,16},{10,18},{12,20},{14,22},{16,24},... | collective-permute-start | bytes 1769480 | tf_op jit(solution)/shard_map/ppermute | solution.py:12
  10.4 5.3 %collective-permute-start.1 = (bf16[2,128,1152]{2,1,0:T(8,128)(2,1)S(1)}, bf16[2,128,1152]{2,1,0:T(8,128)(2,1)S(1)}, u32[]{:S(2)}, u32[]{:S(2)}) collective-permute-start(bf16[2,128,1152]{2,1,0:T(8,128)(2,1)S(1)} %pad_maximum_fusion.1), channel_id=1, source_target_pairs={{0,6},{2,8},{4,10},{6,12},{8,14},{10,16},{12,18},{14,20},{16,22},{... | collective-permute-start | bytes 1769480 | tf_op jit(solution)/shard_map/ppermute | solution.py:12
  15.7 3.2 %collective-permute-start.2 = (bf16[2,128,1152]{2,1,0:T(8,128)(2,1)S(1)}, bf16[2,128,1152]{2,1,0:T(8,128)(2,1)S(1)}, u32[]{:S(2)}, u32[]{:S(2)}) collective-permute-start(bf16[2,128,1152]{2,1,0:T(8,128)(2,1)S(1)} %pad_maximum_fusion.1), channel_id=1, source_target_pairs={{0,4},{2,6},{4,8},{6,10},{8,12},{10,14},{12,16},{14,18},{16,20},{1... | collective-permute-start | bytes 1769480 | tf_op jit(solution)/shard_map/ppermute | solution.py:12
  18.9 1.9 collective-permute-start.3
  20.8 2.4 collective-permute-start.4
  23.3 0.7 abs_compare_fusion
  23.9 0.1 broadcast_and_fusion
  24.0 2.8 broadcast_select_fusion
  26.9 1.3 collective-permute-start.5
  28.2 6.8 %collective-permute-done.1 = bf16[2,128,1152]{2,1,0:T(8,128)(2,1)S(1)} collective-permute-done((bf16[2,128,1152]{2,1,0:T(8,128)(2,1)S(1)}, bf16[2,128,1152]{2,1,0:T(8,128)(2,1)S(1)}, u32[]{:S(2)}, u32[]{:S(2)}) %collective-permute-start.1) | collective-permute-done | bytes 589856 | tf_op jit(solution)/shard_map/ppermute | solution.py:12
  35.0 1.3 collective-permute-start.6
  36.4 11.3 %collective-permute-done.2 = bf16[2,128,1152]{2,1,0:T(8,128)(2,1)S(1)} collective-permute-done((bf16[2,128,1152]{2,1,0:T(8,128)(2,1)S(1)}, bf16[2,128,1152]{2,1,0:T(8,128)(2,1)S(1)}, u32[]{:S(2)}, u32[]{:S(2)}) %collective-permute-start.2) | collective-permute-done | bytes 589856 | tf_op jit(solution)/shard_map/ppermute | solution.py:12
  47.7 1.3 collective-permute-start.7
  49.0 8.8 %collective-permute-done.3 = bf16[2,128,1152]{2,1,0:T(8,128)(2,1)S(1)} collective-permute-done((bf16[2,128,1152]{2,1,0:T(8,128)(2,1)S(1)}, bf16[2,128,1152]{2,1,0:T(8,128)(2,1)S(1)}, u32[]{:S(2)}, u32[]{:S(2)}) %collective-permute-start.3) | collective-permute-done | bytes 589856 | tf_op jit(solution)/shard_map/ppermute | solution.py:12
  58.0 14.6 %collective-permute-done.6 = bf16[2,128,1152]{2,1,0:T(8,128)(2,1)S(1)} collective-permute-done((bf16[2,128,1152]{2,1,0:T(8,128)(2,1)S(1)}, bf16[2,128,1152]{2,1,0:T(8,128)(2,1)S(1)}, u32[]{:S(2)}, u32[]{:S(2)}) %collective-permute-start.6) | collective-permute-done | bytes 589856 | tf_op jit(solution)/shard_map/ppermute | solution.py:12
  73.3 0.6 copy-done.2
  74.0 0.1 copy-done.3
  74.0 0.1 fusion.8
  74.2 0.1 pad_dynamic-update-slice_fusion.3
  74.4 8.5 %convolution_convert_fusion.2 = bf16[2048,1152]{1,0:T(8,128)(2,1)} fusion(bf16[2048,1152]{1,0:T(8,128)(2,1)S(1)} %bitcast.61, bf16[1152,1152]{1,0:T(8,128)(2,1)S(1)} %pad_dynamic-update-slice_fusion.8), kind=kOutput, calls=%fused_computation.4 | convolution fusion | flops 5438177280 | bytes 12091392 | tf_op jit(solution)/shard_map/dot_general | solution.py:84
  83.0 8.3 %pad_maximum_fusion = bf16[2,16,128,1152]{3,2,1,0:T(8,128)(2,1)} fusion(bf16[1,16,128,1152]{3,2,1,0:T(8,128)(2,1)} %bitcast.60), kind=kLoop, calls=%fused_computation.2 | loop fusion | flops 4718592 | bytes 14155776 | tf_op jit(solution)/shard_map/stack | solution.py:88
  91.3 7.3 %all-to-all-start = ((bf16[2,16,128,1152]{3,2,1,0:T(8,128)(2,1)}), bf16[2,16,128,1152]{3,2,1,0:T(8,128)(2,1)}, u32[]{:S(2)}, u32[]{:S(2)}) async-start(bf16[2,16,128,1152]{3,2,1,0:T(8,128)(2,1)} %pad_maximum_fusion), calls=%async_computation | async-start | bytes 18874368 | tf_op jit(solution)/shard_map/all_to_all | solution.py:87
  98.7 0.8 pad_dynamic-update-slice_fusion.2
  99.5 0.7 pad_dynamic-update-slice_fusion.1
  100.2 0.7 pad_dynamic-update-slice_fusion
  100.9 10.9 %convolution_convert_fusion.1 = bf16[2048,1152]{1,0:T(8,128)(2,1)} fusion(bf16[2048,1152]{1,0:T(8,128)(2,1)} %bitcast.62, bf16[1152,1152]{1,0:T(8,128)(2,1)} %pad_dynamic-update-slice_fusion), kind=kOutput, calls=%fused_computation.3 | convolution fusion | flops 5438177280 | bytes 12091392 | tf_op jit(solution)/shard_map/dot_general | solution.py:82
  111.8 5.2 %reshape.77 = bf16[16,147456]{1,0:T(8,128)(2,1)} reshape(bf16[2048,1152]{1,0:T(8,128)(2,1)} %convolution_convert_fusion.1) | data formatting | bytes 9437184 | tf_op jit(solution)/shard_map/reshape | solution.py:83
  117.0 80.1 %all-to-all-done = bf16[2,16,128,1152]{3,2,1,0:T(8,128)(2,1)} async-done(((bf16[2,16,128,1152]{3,2,1,0:T(8,128)(2,1)}), bf16[2,16,128,1152]{3,2,1,0:T(8,128)(2,1)}, u32[]{:S(2)}, u32[]{:S(2)}) %all-to-all-start) | async-done | bytes 9437216 | tf_op jit(solution)/shard_map/all_to_all | solution.py:87
  197.1 12.7 %copy.10 = bf16[4,8,128,1152]{3,1,2,0:T(8,128)(2,1)} copy(bf16[4,8,128,1152]{3,2,1,0:T(8,128)(2,1)} %bitcast.24) | data formatting | bytes 18874368
  209.8 7.2 %fusion = bf16[16,147456]{1,0:T(8,128)(2,1)} fusion(bf16[16,32]{1,0:T(8,128)(2,1)S(1)} %copy-done, bf16[32,147456]{1,0:T(8,128)(2,1)} %bitcast.56), kind=kOutput, calls=%fused_computation.1 | convolution fusion | flops 153354240 | bytes 14156800 | tf_op jit(solution)/shard_map/dot_general | solution.py:101
  217.0 5.3 %reshape.75 = bf16[2048,1152]{1,0:T(8,128)(2,1)} reshape(bf16[16,147456]{1,0:T(8,128)(2,1)} %fusion) | data formatting | bytes 9437184 | tf_op jit(solution)/shard_map/reshape | solution.py:106
  222.3 12.6 %fusion.17 = (bf16[1152,1152]{1,0:T(8,128)(2,1)S(1)}, f32[1152,1152]{1,0:T(8,128)}) fusion(bf16[2048,1152]{1,0:T(8,128)(2,1)} %bitcast.63, bf16[2048,1152]{1,0:T(8,128)(2,1)} %reshape.75), kind=kOutput, calls=%fused_computation.68 | convolution fusion | flops 5437145088 | bytes 17399808 | tf_op jit(solution)/shard_map/dot_general | solution.py:107
  235.0 8.5 %collective-permute-start.11 = (bf16[128,1152]{1,0:T(8,128)(2,1)S(1)}, bf16[128,1152]{1,0:T(8,128)(2,1)S(1)}, u32[]{:S(2)}, u32[]{:S(2)}) collective-permute-start(bf16[128,1152]{1,0:T(8,128)(2,1)S(1)} %concatenate.90), channel_id=1, source_target_pairs={{2,0},{4,2},{6,4},{8,6},{10,8},{12,10},{14,12},{16,14},{18,16},{20... | collective-permute-start | bytes 884744 | tf_op jit(solution)/shard_map/ppermute | solution.py:12
  243.5 3.8 %collective-permute-start.12 = (bf16[128,1152]{1,0:T(8,128)(2,1)S(1)}, bf16[128,1152]{1,0:T(8,128)(2,1)S(1)}, u32[]{:S(2)}, u32[]{:S(2)}) collective-permute-start(bf16[128,1152]{1,0:T(8,128)(2,1)S(1)} %concatenate.91), channel_id=1, source_target_pairs={{0,2},{2,4},{4,6},{6,8},{8,10},{10,12},{12,14},{14,16},{16,18},{18... | collective-permute-start | bytes 884744 | tf_op jit(solution)/shard_map/ppermute | solution.py:12
  247.3 1.3 collective-permute-start.10
  248.7 0.7 concatenate.92
  249.4 4.3 %collective-permute-start.13 = (bf16[128,1152]{1,0:T(8,128)(2,1)}, bf16[128,1152]{1,0:T(8,128)(2,1)S(1)}, u32[]{:S(2)}, u32[]{:S(2)}) collective-permute-start(bf16[128,1152]{1,0:T(8,128)(2,1)} %concatenate.92), channel_id=1, source_target_pairs={{0,4},{2,6},{4,8},{6,10},{8,12},{10,14},{12,16},{14,18},{16,20},{1... | collective-permute-start | bytes 884744 | tf_op jit(solution)/shard_map/ppermute | solution.py:12
  253.8 0.7 concatenate.93
  254.5 4.7 %collective-permute-start.14 = (bf16[128,1152]{1,0:T(8,128)(2,1)}, bf16[128,1152]{1,0:T(8,128)(2,1)S(1)}, u32[]{:S(2)}, u32[]{:S(2)}) collective-permute-start(bf16[128,1152]{1,0:T(8,128)(2,1)} %concatenate.93), channel_id=1, source_target_pairs={{0,6},{2,8},{4,10},{6,12},{8,14},{10,16},{12,18},{14,20},{16,22},{... | collective-permute-start | bytes 884744 | tf_op jit(solution)/shard_map/ppermute | solution.py:12
  259.2 0.7 concatenate.88
  260.0 0.7 concatenate.94
  260.7 0.7 concatenate.87
  261.5 1.3 collective-permute-start.9
  262.8 4.3 %collective-permute-start.15 = (bf16[128,1152]{1,0:T(8,128)(2,1)}, bf16[128,1152]{1,0:T(8,128)(2,1)S(1)}, u32[]{:S(2)}, u32[]{:S(2)}) collective-permute-start(bf16[128,1152]{1,0:T(8,128)(2,1)} %concatenate.94), channel_id=1, source_target_pairs={{0,8},{2,10},{4,12},{6,14},{8,16},{10,18},{12,20},{14,22},{16,24},... | collective-permute-start | bytes 884744 | tf_op jit(solution)/shard_map/ppermute | solution.py:12
  267.1 1.3 collective-permute-start.8
  268.4 4.3 %fusion.18 = f32[16,32]{1,0:T(8,128)S(1)} fusion(bf16[16,147456]{1,0:T(8,128)(2,1)} %reshape.77, bf16[32,147456]{1,0:T(8,128)(2,1)S(1)} %bitcast.59), kind=kOutput, calls=%fused_computation.69 | convolution fusion | flops 150994944 | bytes 14157824 | tf_op jit(solution)/shard_map/dot_general | solution.py:97
  272.8 0.9 reshape.78
  273.7 19.4 %all-to-all-start.2 = ((f32[64,1,512]{2,1,0:T(1,128)}), f32[64,1,512]{2,1,0:T(1,128)S(1)}, u32[]{:S(2)}, u32[]{:S(2)}) async-start(f32[64,1,512]{2,1,0:T(1,128)} %reshape.78), calls=%async_computation.2 | async-start | bytes 262144 | tf_op jit(solution)/shard_map/all_to_all | solution.py:17
  293.2 2.2 fusion.7
  295.4 7.7 %all-to-all-done.2 = f32[64,1,512]{2,1,0:T(1,128)S(1)} async-done(((f32[64,1,512]{2,1,0:T(1,128)}), f32[64,1,512]{2,1,0:T(1,128)S(1)}, u32[]{:S(2)}, u32[]{:S(2)}) %all-to-all-start.2) | async-done | bytes 131104 | tf_op jit(solution)/shard_map/all_to_all | solution.py:17
  303.2 3.5 %all-to-all-start.1 = ((f32[2,64,1152]{2,1,0:T(8,128)}), f32[2,64,1152]{2,1,0:T(8,128)S(1)}, u32[]{:S(2)}, u32[]{:S(2)}) async-start(f32[2,64,1152]{2,1,0:T(8,128)} %bitcast.14), calls=%async_computation.1 | async-start | bytes 1179648 | tf_op jit(solution)/shard_map/all_to_all | solution.py:34
  306.7 0.5 broadcast.96
  307.2 1.0 reduce
  308.1 0.2 reshape.79
  308.3 0.1 reduce_sum.39
  308.4 0.6 broadcast_multiply_fusion
  309.0 6.0 %all-to-all-done.1 = f32[2,64,1152]{2,1,0:T(8,128)S(1)} async-done(((f32[2,64,1152]{2,1,0:T(8,128)}), f32[2,64,1152]{2,1,0:T(8,128)S(1)}, u32[]{:S(2)}, u32[]{:S(2)}) %all-to-all-start.1) | async-done | bytes 589856 | tf_op jit(solution)/shard_map/all_to_all | solution.py:34
  315.1 0.7 select_multiply_fusion
  (72 shorter events, 1.3 us)
Async XLA Ops:
  0.6 209.2 %copy-start = (bf16[16,32]{1,0:T(8,128)(2,1)S(1)}, bf16[16,32]{1,0:T(8,128)(2,1)}, u32[]{:S(2)}) copy-start(bf16[16,32]{1,0:T(8,128)(2,1)} %param.9) | copy-start | bytes 3076
  4.7 22.1 %collective-permute-start = (bf16[2,128,1152]{2,1,0:T(8,128)(2,1)S(1)}, bf16[2,128,1152]{2,1,0:T(8,128)(2,1)S(1)}, u32[]{:S(2)}, u32[]{:S(2)}) collective-permute-start(bf16[2,128,1152]{2,1,0:T(8,128)(2,1)S(1)} %pad_maximum_fusion.1), channel_id=1, source_target_pairs={{0,8},{2,10},{4,12},{6,14},{8,16},{10,18},{12,20},{14,22},{16,24},... | collective-permute-start | bytes 1769480 | tf_op jit(solution)/shard_map/ppermute | solution.py:12
  10.4 24.6 %collective-permute-start.1 = (bf16[2,128,1152]{2,1,0:T(8,128)(2,1)S(1)}, bf16[2,128,1152]{2,1,0:T(8,128)(2,1)S(1)}, u32[]{:S(2)}, u32[]{:S(2)}) collective-permute-start(bf16[2,128,1152]{2,1,0:T(8,128)(2,1)S(1)} %pad_maximum_fusion.1), channel_id=1, source_target_pairs={{0,6},{2,8},{4,10},{6,12},{8,14},{10,16},{12,18},{14,20},{16,22},{... | collective-permute-start | bytes 1769480 | tf_op jit(solution)/shard_map/ppermute | solution.py:12
  15.7 32.0 %collective-permute-start.2 = (bf16[2,128,1152]{2,1,0:T(8,128)(2,1)S(1)}, bf16[2,128,1152]{2,1,0:T(8,128)(2,1)S(1)}, u32[]{:S(2)}, u32[]{:S(2)}) collective-permute-start(bf16[2,128,1152]{2,1,0:T(8,128)(2,1)S(1)} %pad_maximum_fusion.1), channel_id=1, source_target_pairs={{0,4},{2,6},{4,8},{6,10},{8,12},{10,14},{12,16},{14,18},{16,20},{1... | collective-permute-start | bytes 1769480 | tf_op jit(solution)/shard_map/ppermute | solution.py:12
  18.9 38.9 %collective-permute-start.3 = (bf16[2,128,1152]{2,1,0:T(8,128)(2,1)S(1)}, bf16[2,128,1152]{2,1,0:T(8,128)(2,1)S(1)}, u32[]{:S(2)}, u32[]{:S(2)}) collective-permute-start(bf16[2,128,1152]{2,1,0:T(8,128)(2,1)S(1)} %pad_maximum_fusion.1), channel_id=1, source_target_pairs={{0,2},{2,4},{4,6},{6,8},{8,10},{10,12},{12,14},{14,16},{16,18},{18... | collective-permute-start | bytes 1769480 | tf_op jit(solution)/shard_map/ppermute | solution.py:12
  20.8 37.0 %collective-permute-start.4 = (bf16[2,128,1152]{2,1,0:T(8,128)(2,1)S(1)}, bf16[2,128,1152]{2,1,0:T(8,128)(2,1)S(1)}, u32[]{:S(2)}, u32[]{:S(2)}) collective-permute-start(bf16[2,128,1152]{2,1,0:T(8,128)(2,1)S(1)} %pad_maximum_fusion.1), channel_id=1, source_target_pairs={{2,0},{4,2},{6,4},{8,6},{10,8},{12,10},{14,12},{16,14},{18,16},{20... | collective-permute-start | bytes 1769480 | tf_op jit(solution)/shard_map/ppermute | solution.py:12
  26.8 47.6 %copy-start.1 = (bf16[16,128,1152]{2,1,0:T(8,128)(2,1)}, bf16[16,128,1152]{2,1,0:T(8,128)(2,1)S(1)}, u32[]{:S(2)}) copy-start(bf16[16,128,1152]{2,1,0:T(8,128)(2,1)S(1)} %broadcast_select_fusion) | copy-start | bytes 14155780
  26.9 31.0 %collective-permute-start.5 = (bf16[2,128,1152]{2,1,0:T(8,128)(2,1)S(1)}, bf16[2,128,1152]{2,1,0:T(8,128)(2,1)S(1)}, u32[]{:S(2)}, u32[]{:S(2)}) collective-permute-start(bf16[2,128,1152]{2,1,0:T(8,128)(2,1)S(1)} %pad_maximum_fusion.1), channel_id=1, source_target_pairs={{4,0},{6,2},{8,4},{10,6},{12,8},{14,10},{16,12},{18,14},{20,16},{2... | collective-permute-start | bytes 1769480 | tf_op jit(solution)/shard_map/ppermute | solution.py:12
  35.0 37.6 %collective-permute-start.6 = (bf16[2,128,1152]{2,1,0:T(8,128)(2,1)S(1)}, bf16[2,128,1152]{2,1,0:T(8,128)(2,1)S(1)}, u32[]{:S(2)}, u32[]{:S(2)}) collective-permute-start(bf16[2,128,1152]{2,1,0:T(8,128)(2,1)S(1)} %pad_maximum_fusion.1), channel_id=1, source_target_pairs={{6,0},{8,2},{10,4},{12,6},{14,8},{16,10},{18,12},{20,14},{22,16},{... | collective-permute-start | bytes 1769480 | tf_op jit(solution)/shard_map/ppermute | solution.py:12
  47.7 25.4 %collective-permute-start.7 = (bf16[2,128,1152]{2,1,0:T(8,128)(2,1)S(1)}, bf16[2,128,1152]{2,1,0:T(8,128)(2,1)S(1)}, u32[]{:S(2)}, u32[]{:S(2)}) collective-permute-start(bf16[2,128,1152]{2,1,0:T(8,128)(2,1)S(1)} %pad_maximum_fusion.1), channel_id=1, source_target_pairs={{8,0},{10,2},{12,4},{14,6},{16,8},{18,10},{20,12},{22,14},{24,16},... | collective-permute-start | bytes 1769480 | tf_op jit(solution)/shard_map/ppermute | solution.py:12
  73.0 1.0 copy-start.2
  73.0 1.0 copy-start.3
  74.3 8.7 %copy-start.4 = (bf16[1152,1152]{1,0:T(8,128)(2,1)}, bf16[1152,1152]{1,0:T(8,128)(2,1)S(1)}, u32[]{:S(2)}) copy-start(bf16[1152,1152]{1,0:T(8,128)(2,1)S(1)} %get-tuple-element.32) | copy-start | bytes 7962628
  91.3 105.8 %all-to-all-start = ((bf16[2,16,128,1152]{3,2,1,0:T(8,128)(2,1)}), bf16[2,16,128,1152]{3,2,1,0:T(8,128)(2,1)}, u32[]{:S(2)}, u32[]{:S(2)}) async-start(bf16[2,16,128,1152]{3,2,1,0:T(8,128)(2,1)} %pad_maximum_fusion), calls=%async_computation | async-start | bytes 18874368 | tf_op jit(solution)/shard_map/all_to_all | solution.py:87
  217.0 51.4 %slice-start = ((s8[9437184]{0:T(1024)(128)(4,1)}), s8[1048576]{0:T(1024)(128)(4,1)S(1)}, s32[]{:S(2)}) async-start(s8[9437184]{0:T(1024)(128)(4,1)} %bitcast.57), calls=%async_computation.3 | async-start | bytes 2097152
  222.3 46.1 %slice-start.1 = ((s8[9437184]{0:T(1024)(128)(4,1)}), s8[4194304]{0:T(1024)(128)(4,1)S(1)}, s32[]{:S(2)}) async-start(s8[9437184]{0:T(1024)(128)(4,1)} %bitcast.57), calls=%async_computation.4 | async-start | bytes 8388608
  222.3 46.1 %slice-start.2 = ((s8[9437184]{0:T(1024)(128)(4,1)}), s8[4194304]{0:T(1024)(128)(4,1)S(1)}, s32[]{:S(2)}) async-start(s8[9437184]{0:T(1024)(128)(4,1)} %bitcast.57), calls=%async_computation.5 | async-start | bytes 8388608
  235.0 26.4 %collective-permute-start.11 = (bf16[128,1152]{1,0:T(8,128)(2,1)S(1)}, bf16[128,1152]{1,0:T(8,128)(2,1)S(1)}, u32[]{:S(2)}, u32[]{:S(2)}) collective-permute-start(bf16[128,1152]{1,0:T(8,128)(2,1)S(1)} %concatenate.90), channel_id=1, source_target_pairs={{2,0},{4,2},{6,4},{8,6},{10,8},{12,10},{14,12},{16,14},{18,16},{20... | collective-permute-start | bytes 884744 | tf_op jit(solution)/shard_map/ppermute | solution.py:12
  243.5 19.2 %collective-permute-start.12 = (bf16[128,1152]{1,0:T(8,128)(2,1)S(1)}, bf16[128,1152]{1,0:T(8,128)(2,1)S(1)}, u32[]{:S(2)}, u32[]{:S(2)}) collective-permute-start(bf16[128,1152]{1,0:T(8,128)(2,1)S(1)} %concatenate.91), channel_id=1, source_target_pairs={{0,2},{2,4},{4,6},{6,8},{8,10},{10,12},{12,14},{14,16},{16,18},{18... | collective-permute-start | bytes 884744 | tf_op jit(solution)/shard_map/ppermute | solution.py:12
  247.3 19.7 %collective-permute-start.10 = (bf16[128,1152]{1,0:T(8,128)(2,1)S(1)}, bf16[128,1152]{1,0:T(8,128)(2,1)S(1)}, u32[]{:S(2)}, u32[]{:S(2)}) collective-permute-start(bf16[128,1152]{1,0:T(8,128)(2,1)S(1)} %concatenate.89), channel_id=1, source_target_pairs={{4,0},{6,2},{8,4},{10,6},{12,8},{14,10},{16,12},{18,14},{20,16},{2... | collective-permute-start | bytes 884744 | tf_op jit(solution)/shard_map/ppermute | solution.py:12
  249.4 43.8 %collective-permute-start.13 = (bf16[128,1152]{1,0:T(8,128)(2,1)}, bf16[128,1152]{1,0:T(8,128)(2,1)S(1)}, u32[]{:S(2)}, u32[]{:S(2)}) collective-permute-start(bf16[128,1152]{1,0:T(8,128)(2,1)} %concatenate.92), channel_id=1, source_target_pairs={{0,4},{2,6},{4,8},{6,10},{8,12},{10,14},{12,16},{14,18},{16,20},{1... | collective-permute-start | bytes 884744 | tf_op jit(solution)/shard_map/ppermute | solution.py:12
  254.5 38.7 %collective-permute-start.14 = (bf16[128,1152]{1,0:T(8,128)(2,1)}, bf16[128,1152]{1,0:T(8,128)(2,1)S(1)}, u32[]{:S(2)}, u32[]{:S(2)}) collective-permute-start(bf16[128,1152]{1,0:T(8,128)(2,1)} %concatenate.93), channel_id=1, source_target_pairs={{0,6},{2,8},{4,10},{6,12},{8,14},{10,16},{12,18},{14,20},{16,22},{... | collective-permute-start | bytes 884744 | tf_op jit(solution)/shard_map/ppermute | solution.py:12
  261.5 31.7 %collective-permute-start.9 = (bf16[128,1152]{1,0:T(8,128)(2,1)}, bf16[128,1152]{1,0:T(8,128)(2,1)S(1)}, u32[]{:S(2)}, u32[]{:S(2)}) collective-permute-start(bf16[128,1152]{1,0:T(8,128)(2,1)} %concatenate.88), channel_id=1, source_target_pairs={{6,0},{8,2},{10,4},{12,6},{14,8},{16,10},{18,12},{20,14},{22,16},{... | collective-permute-start | bytes 884744 | tf_op jit(solution)/shard_map/ppermute | solution.py:12
  262.8 30.4 %collective-permute-start.15 = (bf16[128,1152]{1,0:T(8,128)(2,1)}, bf16[128,1152]{1,0:T(8,128)(2,1)S(1)}, u32[]{:S(2)}, u32[]{:S(2)}) collective-permute-start(bf16[128,1152]{1,0:T(8,128)(2,1)} %concatenate.94), channel_id=1, source_target_pairs={{0,8},{2,10},{4,12},{6,14},{8,16},{10,18},{12,20},{14,22},{16,24},... | collective-permute-start | bytes 884744 | tf_op jit(solution)/shard_map/ppermute | solution.py:12
  267.1 26.1 %collective-permute-start.8 = (bf16[128,1152]{1,0:T(8,128)(2,1)}, bf16[128,1152]{1,0:T(8,128)(2,1)S(1)}, u32[]{:S(2)}, u32[]{:S(2)}) collective-permute-start(bf16[128,1152]{1,0:T(8,128)(2,1)} %concatenate.87), channel_id=1, source_target_pairs={{8,0},{10,2},{12,4},{14,6},{16,8},{18,10},{20,12},{22,14},{24,16},... | collective-permute-start | bytes 884744 | tf_op jit(solution)/shard_map/ppermute | solution.py:12
  273.7 29.4 %all-to-all-start.2 = ((f32[64,1,512]{2,1,0:T(1,128)}), f32[64,1,512]{2,1,0:T(1,128)S(1)}, u32[]{:S(2)}, u32[]{:S(2)}) async-start(f32[64,1,512]{2,1,0:T(1,128)} %reshape.78), calls=%async_computation.2 | async-start | bytes 262144 | tf_op jit(solution)/shard_map/all_to_all | solution.py:17
  303.2 11.9 %all-to-all-start.1 = ((f32[2,64,1152]{2,1,0:T(8,128)}), f32[2,64,1152]{2,1,0:T(8,128)S(1)}, u32[]{:S(2)}, u32[]{:S(2)}) async-start(f32[2,64,1152]{2,1,0:T(8,128)} %bitcast.14), calls=%async_computation.1 | async-start | bytes 1179648 | tf_op jit(solution)/shard_map/all_to_all | solution.py:34
